TPU v7x, 32 devices: a whole 2x2x4 slice. The times are simulated.
32 devices in a mesh: section: 2 (over core), dp: 4 (over z), tensor: 4 (over y, x).
Axes of the slice: x: 2, y: 2, z: 4, core: 2. Of those that a mesh axis runs over, the one named last changes fastest.
Arguments:
- inputs: bfloat16 [2, 4, 1024, 768], P(None, 'dp', 'tensor'), may hold values from -6 to 6
- segment_ids: int32 [2, 4, 1024], P(None, 'dp'), may hold values from 0 to 7, never falling along the last dimension, each value on 1 to 384 neighbouring positions
- cotangent: float32 [2, 4, 1024, 768], P(None, 'dp', 'tensor'), may hold values from -6 to 6
- qkv_weight: bfloat16 [2, 3, 768, 768], P('section', None, 'dp', 'tensor'), may hold values from -0.21875 to 0.21875
- out_weight: bfloat16 [2, 768, 768], P('section', 'tensor', 'dp'), may hold values from -0.875 to 0.875
- up_weight: bfloat16 [2, 768, 3072], P('section', 'dp', 'tensor'), may hold values from -0.21875 to 0.21875
- down_weight: bfloat16 [2, 3072, 768], P('section', 'tensor', 'dp'), may hold values from -0.109375 to 0.109375
- norm_gain: float32 [2, 2, 768], P('section'), may hold values from 0.5 to 1.5
- norm_bias: float32 [2, 2, 768], P('section'), may hold values from -4 to 4
- qv_bias: float32 [2, 2, 768], P('section'), may hold values from -6 to 6
- up_bias: float32 [2, 3072], P('section'), may hold values from -6 to 6
- resid_bias: float32 [2, 768], P('section'), may hold values from -6 to 6
Outputs:
- outputs: float32 [2, 2, 4, 1024, 768], P('section', None, 'dp', 'tensor')
- input_grads: float32 [2, 2, 4, 1024, 768], P('section', None, 'dp', 'tensor')
- qkv_grad: float32 [2, 3, 768, 768], P('section', None, 'dp', 'tensor')
- out_grad: float32 [2, 768, 768], P('section', 'tensor', 'dp')
- up_grad: float32 [2, 768, 3072], P('section', 'dp', 'tensor')
- down_grad: float32 [2, 3072, 768], P('section', 'tensor', 'dp')
- gain_grad: float32 [2, 2, 768], P('section')
- norm_bias_grad: float32 [2, 2, 768], P('section')
- qv_bias_grad: float32 [2, 2, 768], P('section')
- up_bias_grad: float32 [2, 3072], P('section')
- resid_bias_grad: float32 [2, 768], P('section')
Inputs may be any that keep to these rules, and one draw needn't show every extreme that they name: `segment_ids`: along each sequence the ids never fall; every id 0 to 7 holds 1 to 384 tokens, one of them exactly 384.
All inputs are finite; a program needn't handle non-finite values.
Results may differ from a plain program's by a relative error of at most 0.012.
Values may be sent and summed in bfloat16 or wider, within the bound.
A program may use at most 256 MiB of HBM per device.

v0:
```python
import math

import jax
import jax.numpy as jnp
from jax import lax
from jax.sharding import PartitionSpec as P

HEAD_DIM = 64
ROT = 16


epsilon = 1e-05
root_half = 0.7071067811865476
inv_root_tau = 0.3989422804014327
masked_score = -1e30


def passed_along(block, axis, distance):
    devices = range(lax.axis_size(axis))
    route = [(i - distance, i) for i in devices if i - distance in devices]
    return lax.ppermute(block, axis, route)


def normalize(values, gain_row, shift_row):
    centre = jnp.mean(values, axis=-1, keepdims=True)
    centred = values - centre
    inverse = lax.rsqrt(jnp.mean(centred * centred, axis=-1, keepdims=True) + epsilon)
    unit_rows = centred * inverse
    return (unit_rows, inverse, unit_rows * gain_row + shift_row)


def normalize_back(incoming, unit_rows, inverse, gain_row):
    scaled = incoming * gain_row
    return inverse * (
        scaled
        - jnp.mean(scaled, axis=-1, keepdims=True)
        - unit_rows * jnp.mean(scaled * unit_rows, axis=-1, keepdims=True)
    )


def gelu_value(values):
    return values * 0.5 * (1.0 + lax.erf(values * root_half))


def gelu_slope(values):
    return 0.5 * (1.0 + lax.erf(values * root_half)) + values * inv_root_tau * jnp.exp(
        -0.5 * values * values
    )


def rotary_tables(length, rotated):
    positions = lax.broadcasted_iota(jnp.float32, (length, rotated // 2), 0)
    orders = lax.broadcasted_iota(jnp.float32, (length, rotated // 2), 1)
    angles = positions * jnp.exp(orders * (-2.0 * math.log(10000.0) / rotated))
    return (jnp.cos(angles), jnp.sin(angles))


def rotate(head_vals, cosine_table, sine_table, direction):
    half_rot = cosine_table.shape[-1]
    lower_part = head_vals[..., :half_rot]
    upper_part = head_vals[..., half_rot : 2 * half_rot]
    turned = direction * sine_table
    return jnp.concatenate(
        [
            lower_part * cosine_table - upper_part * turned,
            upper_part * cosine_table + lower_part * turned,
            head_vals[..., 2 * half_rot :],
        ],
        axis=-1,
    )


def score_block(query_part, key_b, segments, offset):
    row_count = query_part.shape[1]
    length = key_b.shape[1]
    scores = jnp.einsum("sqhd,skhd->shqk", query_part, key_b, preferred_element_type=jnp.float32)
    query_pos = lax.broadcasted_iota(jnp.int32, (row_count, length), 0) + offset
    key_pos = lax.broadcasted_iota(jnp.int32, (row_count, length), 1)
    same_doc = segments[:, offset : offset + row_count][:, :, None] == segments[:, None, :]
    allowed = same_doc & (key_pos <= query_pos)[None]
    return jnp.where(allowed[:, None], scores, masked_score)


def attend(query_b, key_b, value_b, segments):
    length = query_b.shape[1]
    block_rows = min(512, length)
    contexts = []
    log_totals = []
    for offset in range(0, length, block_rows):
        scores = score_block(query_b[:, offset : offset + block_rows], key_b, segments, offset)
        row_top = jnp.max(scores, axis=-1, keepdims=True)
        log_total = row_top + jnp.log(jnp.sum(jnp.exp(scores - row_top), axis=-1, keepdims=True))
        probs_b = jnp.exp(scores - log_total).astype(jnp.bfloat16)
        contexts.append(
            jnp.einsum(
                "shqk,skhd->sqhd", probs_b, value_b, preferred_element_type=jnp.float32
            ).astype(jnp.bfloat16)
        )
        log_totals.append(log_total)
    return (jnp.concatenate(contexts, axis=1), jnp.concatenate(log_totals, axis=2))


def attend_back(query_b, key_b, value_b, segments, log_totals, context_gradient):
    length = query_b.shape[1]
    block_rows = min(512, length)
    key_grad = jnp.zeros(key_b.shape, jnp.float32)
    value_grad = jnp.zeros(value_b.shape, jnp.float32)
    query_parts = []
    for offset in range(0, length, block_rows):
        query_part = query_b[:, offset : offset + block_rows]
        grad_part = context_gradient[:, offset : offset + block_rows]
        scores = score_block(query_part, key_b, segments, offset)
        probs = jnp.exp(scores - log_totals[:, :, offset : offset + block_rows])
        probs_b = probs.astype(jnp.bfloat16)
        value_grad = value_grad + jnp.einsum(
            "shqk,sqhd->skhd", probs_b, grad_part, preferred_element_type=jnp.float32
        )
        prob_grad = jnp.einsum(
            "sqhd,skhd->shqk", grad_part, value_b, preferred_element_type=jnp.float32
        )
        score_grad = probs * (prob_grad - jnp.sum(probs * prob_grad, axis=-1, keepdims=True))
        score_b = score_grad.astype(jnp.bfloat16)
        query_parts.append(
            jnp.einsum("shqk,skhd->sqhd", score_b, key_b, preferred_element_type=jnp.float32)
        )
        key_grad = key_grad + jnp.einsum(
            "shqk,sqhd->skhd", score_b, query_part, preferred_element_type=jnp.float32
        )
    return (jnp.concatenate(query_parts, axis=1), key_grad, value_grad)


def layer_pieces(x_part, segments, weight_matrices, params, cosine_table, sine_table):
    query_key_value_matrix, output_matrix, up_matrix, down_matrix = weight_matrices
    gain_pair, shift_pair, qv_local, up_weight_shard, resid_row = params
    gathered = lax.all_gather(x_part, "tensor", axis=1, tiled=True)
    widened = gathered.astype(jnp.float32)
    unit_one, inverse_one, normed_one = normalize(widened, gain_pair[0], shift_pair[0])
    unit_two, inverse_two, normed_two = normalize(widened, gain_pair[1], shift_pair[1])
    attention_input = normed_one.astype(jnp.bfloat16)
    feedforward_input = normed_two.astype(jnp.bfloat16)
    projected_rows = jnp.einsum(
        "bnp,kpq->kbnq", attention_input, query_key_value_matrix, preferred_element_type=jnp.float32
    )
    seq_count = attention_input.shape[0]
    length = attention_input.shape[1]
    heads_local = query_key_value_matrix.shape[2] // HEAD_DIM
    head_shape = (seq_count, length, heads_local, HEAD_DIM)
    cos_b = cosine_table[None, :, None, :]
    sin_b = sine_table[None, :, None, :]
    query_b = (
        rotate((projected_rows[0] + qv_local[0]).reshape(head_shape), cos_b, sin_b, 1.0) * 0.125
    ).astype(jnp.bfloat16)
    key_b = rotate(projected_rows[1].reshape(head_shape), cos_b, sin_b, 1.0).astype(jnp.bfloat16)
    value_b = (projected_rows[2] + qv_local[1]).reshape(head_shape).astype(jnp.bfloat16)
    context, log_totals = attend(query_b, key_b, value_b, segments)
    up_pre = (
        jnp.einsum("ogu,ui->ogi", feedforward_input, up_matrix, preferred_element_type=jnp.float32)
        + up_weight_shard
    )
    hidden_block = gelu_value(up_pre).astype(jnp.bfloat16)
    return (
        attention_input,
        feedforward_input,
        query_b,
        key_b,
        value_b,
        context,
        log_totals,
        up_pre,
        hidden_block,
        unit_one,
        inverse_one,
        unit_two,
        inverse_two,
    )


def layer_forward(x_part, segments, weight_matrices, params, cosine_table, sine_table):
    pieces = layer_pieces(x_part, segments, weight_matrices, params, cosine_table, sine_table)
    context = pieces[5]
    hidden_block = pieces[8]
    flattened_context = context.reshape(context.shape[0], context.shape[1], -1)
    branch = jnp.einsum(
        "xji,iy->xjy", flattened_context, weight_matrices[1], preferred_element_type=jnp.float32
    ) + jnp.einsum(
        "teo,ov->tev", hidden_block, weight_matrices[3], preferred_element_type=jnp.float32
    )
    summed = lax.psum_scatter(branch, "tensor", scatter_dimension=1, tiled=True)
    return x_part.astype(jnp.float32) + summed + params[4]


def layer_backward(x_part, segments, incoming, weight_matrices, params, cosine_table, sine_table):
    query_key_value_matrix, output_matrix, up_matrix, down_matrix = weight_matrices
    gain_pair, shift_pair, qv_local, up_weight_shard, resid_row = params
    (
        attention_input,
        feedforward_input,
        query_b,
        key_b,
        value_b,
        context,
        log_totals,
        up_pre,
        hidden_block,
        unit_one_all,
        inverse_one_all,
        unit_two_all,
        inverse_two_all,
    ) = layer_pieces(x_part, segments, weight_matrices, params, cosine_table, sine_table)
    seq_count = context.shape[0]
    length = context.shape[1]
    flattened_context = context.reshape(seq_count, length, -1)
    grad_b = incoming.astype(jnp.bfloat16)
    gradient_rows = lax.all_gather(grad_b, "tensor", axis=1, tiled=True)
    down_weight_gradient = jnp.einsum(
        "zca,zck->ak", hidden_block, gradient_rows, preferred_element_type=jnp.float32
    )
    output_weight_gradient = jnp.einsum(
        "afx,afp->xp", flattened_context, gradient_rows, preferred_element_type=jnp.float32
    )
    pre_grad = jnp.einsum(
        "qhi,ji->qhj", gradient_rows, down_matrix, preferred_element_type=jnp.float32
    ) * gelu_slope(up_pre)
    up_bias_g = jnp.sum(pre_grad, axis=(0, 1))
    preactivation_block = pre_grad.astype(jnp.bfloat16)
    up_weight_gradient = jnp.einsum(
        "oec,oep->cp", feedforward_input, preactivation_block, preferred_element_type=jnp.float32
    )
    feedforward_input_gradient = jnp.einsum(
        "gmi,ti->gmt", preactivation_block, up_matrix, preferred_element_type=jnp.float32
    )
    context_gradient = jnp.einsum(
        "cwm,am->cwa", gradient_rows, output_matrix, preferred_element_type=jnp.float32
    )
    context_gradient = context_gradient.astype(jnp.bfloat16).reshape(context.shape)
    query_grad, key_grad, value_grad = attend_back(
        query_b, key_b, value_b, segments, log_totals, context_gradient
    )
    cos_b = cosine_table[None, :, None, :]
    sin_b = sine_table[None, :, None, :]
    query_grad = rotate(query_grad, cos_b, sin_b, -1.0) * 0.125
    key_grad = rotate(key_grad, cos_b, sin_b, -1.0)
    flat_shape = (seq_count, length, flattened_context.shape[2])
    stacked = jnp.stack(
        [
            query_grad.reshape(flat_shape),
            key_grad.reshape(flat_shape),
            value_grad.reshape(flat_shape),
        ]
    )
    qv_g = jnp.stack([jnp.sum(stacked[0], axis=(0, 1)), jnp.sum(stacked[2], axis=(0, 1))])
    stacked_block = stacked.astype(jnp.bfloat16)
    query_key_value_gradient = jnp.einsum(
        "ivw,qivn->qwn", attention_input, stacked_block, preferred_element_type=jnp.float32
    )
    attn_in_grad = jnp.einsum(
        "hria,hoa->rio", stacked_block, query_key_value_matrix, preferred_element_type=jnp.float32
    )
    attn_part, mlp_part = (
        lax.psum_scatter(attn_in_grad, "tensor", scatter_dimension=1, tiled=True),
        lax.psum_scatter(feedforward_input_gradient, "tensor", scatter_dimension=1, tiled=True),
    )
    widened = x_part.astype(jnp.float32)
    unit_one, inverse_one, normed_skip = normalize(widened, gain_pair[0], shift_pair[0])
    unit_two, inverse_two, normed_drop = normalize(widened, gain_pair[1], shift_pair[1])
    gain_g = jnp.stack(
        [jnp.sum(attn_part * unit_one, axis=(0, 1)), jnp.sum(mlp_part * unit_two, axis=(0, 1))]
    )
    shift_g = jnp.stack([jnp.sum(attn_part, axis=(0, 1)), jnp.sum(mlp_part, axis=(0, 1))])
    input_grad = (
        incoming
        + normalize_back(attn_part, unit_one, inverse_one, gain_pair[0])
        + normalize_back(mlp_part, unit_two, inverse_two, gain_pair[1])
    )
    resid_g = jnp.sum(incoming, axis=(0, 1))
    return (
        input_grad,
        (
            query_key_value_gradient,
            output_weight_gradient,
            up_weight_gradient,
            down_weight_gradient,
        ),
        (gain_g, shift_g, qv_g, up_bias_g, resid_g),
    )


def body(
    inputs,
    segment_ids,
    cotangent,
    qkv_weight,
    out_weight,
    up_weight,
    down_weight,
    norm_gain,
    norm_bias,
    qv_bias,
    up_bias,
    resid_bias,
):
    leading = lax.axis_index("section") == 0
    column = lax.axis_index("tensor")
    micro_count = inputs.shape[0]
    head_cols = qkv_weight.shape[3]
    ff_local = up_weight.shape[2]
    qv_local = lax.dynamic_slice_in_dim(qv_bias[0], column * head_cols, head_cols, 1)
    up_weight_shard = lax.dynamic_slice_in_dim(up_bias[0], column * ff_local, ff_local, 0)
    params = (norm_gain[0], norm_bias[0], qv_local, up_weight_shard, resid_bias[0])
    shards = (qkv_weight[0], out_weight[0], up_weight[0], down_weight[0])
    cosine_table, sine_table = rotary_tables(segment_ids.shape[2], ROT)

    def fetch_weights():
        return (
            lax.all_gather(shards[0], "dp", axis=1, tiled=True),
            lax.all_gather(shards[1], "dp", axis=1, tiled=True),
            lax.all_gather(shards[2], "dp", axis=0, tiled=True),
            lax.all_gather(shards[3], "dp", axis=1, tiled=True),
        )

    arriving = jnp.zeros(inputs.shape[1:], jnp.bfloat16)
    seen_inputs = []
    made_outputs = []
    for moment in range(micro_count + 1):
        current = min(moment, micro_count - 1)
        earlier = max(moment - 1, 0)
        layer_in = jnp.where(leading, inputs[current], arriving)
        layer_seg = jnp.where(leading, segment_ids[current], segment_ids[earlier])
        weight_matrices = fetch_weights()
        layer_wide = layer_forward(
            layer_in, layer_seg, weight_matrices, params, cosine_table, sine_table
        )
        layer_out = layer_wide.astype(jnp.bfloat16)
        arriving = passed_along(layer_out, "section", 1)
        seen_inputs.append(layer_in)
        made_outputs.append(layer_wide)
    held_inputs = [
        jnp.where(leading, seen_inputs[slot_no], seen_inputs[slot_no + 1])
        for slot_no in range(micro_count)
    ]
    grads_held = tuple((jnp.zeros(piece.shape, jnp.float32) for piece in shards))
    small_held = (
        jnp.zeros(norm_gain.shape[1:], jnp.float32),
        jnp.zeros(norm_bias.shape[1:], jnp.float32),
        jnp.zeros((2, head_cols), jnp.float32),
        jnp.zeros((ff_local,), jnp.float32),
        jnp.zeros(resid_bias.shape[1:], jnp.float32),
    )
    returning = jnp.zeros(cotangent.shape[1:], jnp.float32)
    back_list = []
    for moment in range(micro_count + 1):
        current = min(moment, micro_count - 1)
        earlier = max(moment - 1, 0)
        active = jnp.where(leading, moment >= 1, moment < micro_count).astype(jnp.float32)
        incoming = jnp.where(leading, returning, cotangent[current]) * active
        layer_in = jnp.where(leading, held_inputs[earlier], held_inputs[current])
        layer_seg = jnp.where(leading, segment_ids[earlier], segment_ids[current])
        weight_matrices = fetch_weights()
        input_grad, matrix_grads, small_grads = layer_backward(
            layer_in, layer_seg, incoming, weight_matrices, params, cosine_table, sine_table
        )
        returning = passed_along(input_grad, "section", -1)
        back_list.append(input_grad)
        reduced = (
            lax.psum_scatter(matrix_grads[0], "dp", scatter_dimension=1, tiled=True),
            lax.psum_scatter(matrix_grads[1], "dp", scatter_dimension=1, tiled=True),
            lax.psum_scatter(matrix_grads[2], "dp", scatter_dimension=0, tiled=True),
            lax.psum_scatter(matrix_grads[3], "dp", scatter_dimension=1, tiled=True),
        )
        grads_held = tuple((held + piece for held, piece in zip(grads_held, reduced)))
        small_held = tuple((held + piece for held, piece in zip(small_held, small_grads)))
    qv_full = lax.dynamic_update_slice_in_dim(
        jnp.zeros((2, qv_bias.shape[2]), jnp.float32), small_held[2], column * head_cols, 1
    )
    up_full = lax.dynamic_update_slice_in_dim(
        jnp.zeros((up_bias.shape[1],), jnp.float32), small_held[3], column * ff_local, 0
    )
    totals = lax.psum(
        (small_held[0], small_held[1], qv_full, up_full, small_held[4]), ("dp", "tensor")
    )
    outputs = jnp.stack(
        [
            jnp.where(leading, made_outputs[slot_no], made_outputs[slot_no + 1])
            for slot_no in range(micro_count)
        ]
    )[None]
    input_grads = jnp.stack(
        [
            jnp.where(leading, back_list[slot_no + 1], back_list[slot_no])
            for slot_no in range(micro_count)
        ]
    )[None]
    return (
        outputs,
        input_grads,
        grads_held[0][None],
        grads_held[1][None],
        grads_held[2][None],
        grads_held[3][None],
        totals[0][None],
        totals[1][None],
        totals[2][None],
        totals[3][None],
        totals[4][None],
    )


def solution(mesh):
    return jax.shard_map(
        body,
        mesh=mesh,
        in_specs=(
            P(None, "dp", "tensor", None),
            P(None, "dp", None),
            P(None, "dp", "tensor", None),
            P("section", None, "dp", "tensor"),
            P("section", "tensor", "dp"),
            P("section", "dp", "tensor"),
            P("section", "tensor", "dp"),
            P("section", None, None),
            P("section", None, None),
            P("section", None, None),
            P("section", None),
            P("section", None),
        ),
        out_specs=(
            P("section", None, "dp", "tensor", None),
            P("section", None, "dp", "tensor", None),
            P("section", None, "dp", "tensor"),
            P("section", "tensor", "dp"),
            P("section", "dp", "tensor"),
            P("section", "tensor", "dp"),
            P("section", None, None),
            P("section", None, None),
            P("section", None, None),
            P("section", None),
            P("section", None),
        ),
        check_vma=False,
    )
```

profile of v0, /device:TPU:0, one launch (start us, length us, event | category | flops | bytes accessed | tf_op | source)
XLA Modules:
  0.0 1099.7 jit_solution(5559627993317711063)
XLA Ops:
  17.8 21.3 %all-gather.2 = bf16[1,192,768]{1,0,2:T(2,128)(2,1)S(1)} all-gather(bf16[1,192,192]{1,0,2:T(2,128)(2,1)S(1)} %copy.35), channel_id=4, replica_groups=mesh['section'=2,'dp'=4,'tensor'=4] {'dp'}, dimensions={2}, use_global_device_ids=true | all-gather | bytes 368640 | tf_op jit(solution)/shard_map/all_gather | solution.py:316
  39.6 40.9 %all-gather.1 = bf16[1,3,768,192]{3,1,0,2:T(4,128)(2,1)S(1)} all-gather(bf16[1,3,192,192]{3,1,0,2:T(4,128)(2,1)S(1)} %copy.33), channel_id=3, replica_groups=mesh['section'=2,'dp'=4,'tensor'=4] {'dp'}, dimensions={2}, use_global_device_ids=true | all-gather | bytes 1105920 | tf_op jit(solution)/shard_map/all_gather | solution.py:315
  100.8 16.7 %all-gather.37.cloned.1.call-done = bf16[1,768,768]{1,2,0:T(8,128)(2,1)} async-done(((bf16[1,768,192]{1,2,0:T(8,128)(2,1)}), bf16[1,768,768]{1,2,0:T(8,128)(2,1)}) %all-gather.37.cloned.1.call-update) | async-done | bytes 1179664 | tf_op jit(solution)/shard_map/all_gather | solution.py:318
  117.4 6.6 fusion.206
  124.1 4.2 add_bitcast_fusion.2
  128.9 42.6 %reduce-scatter.18.cloned.1.call-done = f32[1,256,768]{2,1,0:T(8,128)} async-done(((f32[1,1024,768]{2,1,0:T(8,128)}), f32[1,256,768]{2,1,0:T(8,128)}) %reduce-scatter.18.cloned.1.call-update) | async-done | bytes 786448 | tf_op jit(solution)/shard_map/reduce_scatter | solution.py:188
  178.1 29.5 %all-gather.17.cloned.1.call-done = bf16[1,1024,768]{2,1,0:T(8,128)(2,1)} async-done(((bf16[1,256,768]{2,1,0:T(8,128)(2,1)}), bf16[1,1024,768]{2,1,0:T(8,128)(2,1)}) %all-gather.17.cloned.1.call-update) | async-done | bytes 1572880 | tf_op jit(solution)/shard_map/all_gather | solution.py:135
  223.6 6.6 fusion.204
  230.2 4.2 add_bitcast_fusion.1
  237.1 41.3 %reduce-scatter.20.cloned.1.call-done = f32[1,256,768]{2,1,0:T(8,128)} async-done(((f32[1,1024,768]{2,1,0:T(8,128)}), f32[1,256,768]{2,1,0:T(8,128)}) %reduce-scatter.20.cloned.1.call-update) | async-done | bytes 786448 | tf_op jit(solution)/shard_map/reduce_scatter | solution.py:188
  288.7 23.1 %all-gather.23.cloned.1.call-done = bf16[1,1024,768]{2,1,0:T(8,128)(2,1)} async-done(((bf16[1,256,768]{2,1,0:T(8,128)(2,1)}), bf16[1,1024,768]{2,1,0:T(8,128)(2,1)}) %all-gather.23.cloned.1.call-update) | async-done | bytes 1572880 | tf_op jit(solution)/shard_map/all_gather | solution.py:214
  314.8 29.6 %all-gather.29.cloned.1.call-done = bf16[1,1024,768]{2,1,0:T(8,128)(2,1)} async-done(((bf16[1,256,768]{2,1,0:T(8,128)(2,1)}), bf16[1,1024,768]{2,1,0:T(8,128)(2,1)}) %all-gather.29.cloned.1.call-update) | async-done | bytes 1572880 | tf_op jit(solution)/shard_map/all_gather | solution.py:135
  346.1 31.0 %all-gather.19.cloned.1.call-done = bf16[1,1024,768]{2,1,0:T(8,128)(2,1)} async-done(((bf16[1,256,768]{2,1,0:T(8,128)(2,1)}), bf16[1,1024,768]{2,1,0:T(8,128)(2,1)}) %all-gather.19.cloned.1.call-update) | async-done | bytes 1572880 | tf_op jit(solution)/shard_map/all_gather | solution.py:135
  378.8 31.4 %all-gather.21.cloned.1.call-done = bf16[1,1024,768]{2,1,0:T(8,128)(2,1)} async-done(((bf16[1,256,768]{2,1,0:T(8,128)(2,1)}), bf16[1,1024,768]{2,1,0:T(8,128)(2,1)}) %all-gather.21.cloned.1.call-update) | async-done | bytes 1572880 | tf_op jit(solution)/shard_map/all_gather | solution.py:135
  415.6 27.4 %all-gather.25.cloned.1.call-done = bf16[1,1024,768]{2,1,0:T(8,128)(2,1)} async-done(((bf16[1,256,768]{2,1,0:T(8,128)(2,1)}), bf16[1,1024,768]{2,1,0:T(8,128)(2,1)}) %all-gather.25.cloned.1.call-update) | async-done | bytes 1572880 | tf_op jit(solution)/shard_map/all_gather | solution.py:135
  462.4 3.9 select_reduce_fusion.4
  466.3 3.8 select_reduce_fusion.5
  472.0 3.4 fusion.482
  479.7 3.8 exponential_reduce_fusion.4
  483.6 4.0 exponential_reduce_fusion.5
  510.7 13.0 %reduce-scatter.26.cloned.1.call-done = f32[1,256,768]{2,1,0:T(8,128)} async-done(((f32[1,1024,768]{2,1,0:T(8,128)}), f32[1,256,768]{2,1,0:T(8,128)}) %reduce-scatter.26.cloned.1.call-update) | async-done | bytes 786448 | tf_op jit(solution)/shard_map/reduce_scatter | solution.py:261
  523.7 46.9 %reduce-scatter.24.cloned.1.call-done = f32[1,256,768]{2,1,0:T(8,128)} async-done(((f32[1,1024,768]{2,1,0:T(8,128)}), f32[1,256,768]{2,1,0:T(8,128)}) %reduce-scatter.24.cloned.1.call-update) | async-done | bytes 786448 | tf_op jit(solution)/shard_map/reduce_scatter | solution.py:260
  587.9 3.7 fusion.212
  593.2 20.0 %all-gather.27.cloned.1.call-done = bf16[1,1024,768]{2,1,0:T(8,128)(2,1)} async-done(((bf16[1,256,768]{2,1,0:T(8,128)(2,1)}), bf16[1,1024,768]{2,1,0:T(8,128)(2,1)}) %all-gather.27.cloned.1.call-update) | async-done | bytes 1572880 | tf_op jit(solution)/shard_map/all_gather | solution.py:214
  613.2 5.5 fusion.483
  625.3 4.8 multiply_reduce_fusion.3
  672.8 5.2 exponential_reduce_fusion.1
  678.0 5.4 exponential_reduce_fusion
  683.4 30.4 %reduce-scatter.28.cloned.1.call-done = f32[1,256,768]{2,1,0:T(8,128)} async-done(((f32[1,1024,768]{2,1,0:T(8,128)}), f32[1,256,768]{2,1,0:T(8,128)}) %reduce-scatter.28.cloned.1.call-update) | async-done | bytes 786448 | tf_op jit(solution)/shard_map/reduce_scatter | solution.py:260
  721.3 5.2 fusion.232
  731.9 4.6 fusion.236
  745.9 14.8 %all-gather.31.cloned.1.call-done = bf16[1,1024,768]{2,1,0:T(8,128)(2,1)} async-done(((bf16[1,256,768]{2,1,0:T(8,128)(2,1)}), bf16[1,1024,768]{2,1,0:T(8,128)(2,1)}) %all-gather.31.cloned.1.call-update) | async-done | bytes 1572880 | tf_op jit(solution)/shard_map/all_gather | solution.py:214
  762.9 5.4 fusion.357
  768.3 7.2 multiply_reduce_fusion.1
  783.9 7.5 multiply_reduce_fusion
  808.1 3.5 fusion.209
  824.8 6.2 fusion.202
  831.1 4.6 fusion.231
  835.7 4.7 fusion.230
  844.3 3.3 fusion.318
  849.6 3.3 add_add_fusion.1
  852.9 3.7 fusion.93
  859.4 3.3 add_add_fusion
  867.8 28.6 %reduce-scatter.34.cloned.1.call-done = f32[1,256,768]{2,1,0:T(8,128)} async-done(((f32[1,1024,768]{2,1,0:T(8,128)}), f32[1,256,768]{2,1,0:T(8,128)}) %reduce-scatter.34.cloned.1.call-update) | async-done | bytes 786448 | tf_op jit(solution)/shard_map/reduce_scatter | solution.py:261
  896.5 46.9 %reduce-scatter.32.cloned.1.call-done = f32[1,256,768]{2,1,0:T(8,128)} async-done(((f32[1,1024,768]{2,1,0:T(8,128)}), f32[1,256,768]{2,1,0:T(8,128)}) %reduce-scatter.32.cloned.1.call-update) | async-done | bytes 786448 | tf_op jit(solution)/shard_map/reduce_scatter | solution.py:260
  946.1 78.1 %all-reduce = (f32[1,2,768]{2,1,0:T(2,128)}, f32[1,2,768]{2,1,0:T(2,128)}, f32[1,2,768]{2,1,0:T(2,128)}, f32[1,3072]{1,0:T(1,128)}, f32[1,768]{1,0:T(1,128)}) all-reduce(f32[1,2,768]{2,1,0:T(2,128)S(1)} %fusion.405, f32[1,2,768]{2,1,0:T(2,128)S(1)} %fusion.407, ...), channel_id=1, replica_groups=mesh['section'=2,'dp'=4,'tensor'=4] {'dp','tensor'}, use_global_device_ids=true, to_apply=%region_87.88 | all-reduce | flops 8448 | bytes 67584 | tf_op jit(solution)/shard_map/psum | solution.py:378
  1029.3 12.9 %reduce-scatter.36.cloned.1.call-done = f32[192,768]{1,0:T(8,128)} async-done(((f32[768,768]{1,0:T(8,128)}), f32[192,768]{1,0:T(8,128)}) %reduce-scatter.36.cloned.1.call-update) | async-done | bytes 589840 | tf_op jit(solution)/shard_map/reduce_scatter | solution.py:367
  1042.2 50.5 %reduce-scatter.38.cloned.1.call-done = f32[768,192]{0,1:T(8,128)} async-done(((f32[768,768]{0,1:T(8,128)}), f32[768,192]{0,1:T(8,128)}) %reduce-scatter.38.cloned.1.call-update) | async-done | bytes 589840 | tf_op jit(solution)/shard_map/reduce_scatter | solution.py:368
  (855 shorter events, 276.6 us)
Async XLA Ops:
  7.2 74.2 %copy-start = (f32[1,3072]{1,0:T(1,128)S(1)}, f32[1,3072]{1,0:T(1,128)}, u32[]{:S(2)}) copy-start(f32[1,3072]{1,0:T(1,128)} %param.22) | copy-start | bytes 36868
  7.2 78.0 %all-gather.33.cloned.1.call-start = ((), (), s32[]{:S(2)}) async-start(), calls=%async_computation.30 | async-start | bytes 1966080 | tf_op jit(solution)/shard_map/all_gather | solution.py:135
  9.0 91.7 %all-gather.35.cloned.1.call-start = ((), (), s32[]{:S(2)}) async-start(), calls=%async_computation.31 | async-start | bytes 1474560 | tf_op jit(solution)/shard_map/all_gather | solution.py:317
  9.8 107.6 %all-gather.37.cloned.1.call-start = ((), (), s32[]{:S(2)}) async-start(), calls=%async_computation.32 | async-start | bytes 1474560 | tf_op jit(solution)/shard_map/all_gather | solution.py:318
  10.5 161.0 %reduce-scatter.18.cloned.1.call-start = ((), (), s32[]{:S(2)}) async-start(), calls=%async_computation.13 | async-start | bytes 3932160 | tf_op jit(solution)/shard_map/reduce_scatter | solution.py:188
  10.6 166.0 %copy-start.137 = (s32[512]{0:T(512)}, s32[512]{0:T(512)S(1)}, u32[]{:S(2)}) copy-start(s32[512]{0:T(512)S(1)} %iota_add_fusion) | copy-start | bytes 6148
  13.6 85.3 %copy-start.173 = (f32[3,64]{1,0:T(4,128)}, f32[3,64]{1,0:T(4,128)S(1)}, u32[]{:S(2)}) copy-start(f32[3,64]{1,0:T(4,128)S(1)} %add.830) | copy-start | bytes 2308
  14.4 573.0 %copy-start.117 = (f32[768]{0:T(1024)}, f32[768]{0:T(1024)S(1)}, u32[]{:S(2)}) copy-start(f32[768]{0:T(1024)S(1)} %get-tuple-element.91) | copy-start | bytes 9220
  15.3 73.8 %copy-start.189 = (f32[768]{0:T(1024)}, f32[768]{0:T(1024)S(1)}, u32[]{:S(2)}) copy-start(f32[768]{0:T(1024)S(1)} %get-tuple-element.92) | copy-start | bytes 9220
  15.3 102.2 %copy-start.186 = (f32[768]{0:T(1024)}, f32[768]{0:T(1024)S(1)}, u32[]{:S(2)}) copy-start(f32[768]{0:T(1024)S(1)} %get-tuple-element.93) | copy-start | bytes 9220
  15.5 624.5 %copy-start.45 = (f32[1024,8]{0,1:T(8,128)}, f32[1024,8]{0,1:T(8,128)S(1)}, u32[]{:S(2)}) copy-start(f32[1024,8]{0,1:T(8,128)S(1)} %get-tuple-element.239) | copy-start | bytes 98308
  15.5 624.5 %copy-start.76 = (f32[1024,8]{0,1:T(8,128)}, f32[1024,8]{0,1:T(8,128)S(1)}, u32[]{:S(2)}) copy-start(f32[1024,8]{0,1:T(8,128)S(1)} %get-tuple-element.237) | copy-start | bytes 98308
  39.6 84.5 %copy-start.41 = (bf16[1,192,768]{2,1,0:T(8,128)(2,1)}, bf16[1,192,768]{2,1,0:T(8,128)(2,1)S(1)}, u32[]{:S(2)}) copy-start(bf16[1,192,768]{2,1,0:T(8,128)(2,1)S(1)} %copy.36) | copy-start | bytes 884740
  128.2 79.3 %all-gather.17.cloned.1.call-start = ((), (), s32[]{:S(2)}) async-start(), calls=%async_computation.14 | async-start | bytes 1966080 | tf_op jit(solution)/shard_map/all_gather | solution.py:135
  128.9 149.6 %copy-start.127 = (f32[768]{0:T(1024)}, f32[768]{0:T(1024)S(1)}, u32[]{:S(2)}) copy-start(f32[768]{0:T(1024)S(1)} %reduce.114) | copy-start | bytes 9220
  172.8 2.9 collective-permute-start
  176.6 101.9 %reduce-scatter.20.cloned.1.call-start = ((), (), s32[]{:S(2)}) async-start(), calls=%async_computation.15 | async-start | bytes 3932160 | tf_op jit(solution)/shard_map/reduce_scatter | solution.py:188
  234.4 77.3 %all-gather.23.cloned.1.call-start = ((), (), s32[]{:S(2)}) async-start(), calls=%async_computation.19 | async-start | bytes 1966080 | tf_op jit(solution)/shard_map/all_gather | solution.py:214
  237.1 107.4 %all-gather.29.cloned.1.call-start = ((), (), s32[]{:S(2)}) async-start(), calls=%async_computation.26 | async-start | bytes 1966080 | tf_op jit(solution)/shard_map/all_gather | solution.py:135
  281.0 2.9 collective-permute-start.1
  285.0 92.2 %all-gather.19.cloned.1.call-start = ((), (), s32[]{:S(2)}) async-start(), calls=%async_computation.16 | async-start | bytes 1966080 | tf_op jit(solution)/shard_map/all_gather | solution.py:135
  285.7 124.6 %all-gather.21.cloned.1.call-start = ((), (), s32[]{:S(2)}) async-start(), calls=%async_computation.18 | async-start | bytes 1966080 | tf_op jit(solution)/shard_map/all_gather | solution.py:135
  288.6 154.4 %all-gather.25.cloned.1.call-start = ((), (), s32[]{:S(2)}) async-start(), calls=%async_computation.22 | async-start | bytes 1966080 | tf_op jit(solution)/shard_map/all_gather | solution.py:135
  314.6 209.1 %reduce-scatter.26.cloned.1.call-start = ((), (), s32[]{:S(2)}) async-start(), calls=%async_computation.21 | async-start | bytes 3932160 | tf_op jit(solution)/shard_map/reduce_scatter | solution.py:261
  444.8 142.6 %copy-start.160 = (f32[1024]{0:T(1024)}, f32[1024]{0:T(1024)S(1)}, u32[]{:S(2)}) copy-start(f32[1024]{0:T(1024)S(1)} %broadcast_multiply_fusion.2) | copy-start | bytes 12292
  479.6 91.0 %reduce-scatter.24.cloned.1.call-start = ((), (), s32[]{:S(2)}) async-start(), calls=%async_computation.20 | async-start | bytes 3932160 | tf_op jit(solution)/shard_map/reduce_scatter | solution.py:260
  509.3 67.6 %copy-start.68 = (f32[1,1024,3,64]{1,3,2,0:T(8,128)S(1)}, f32[1,1024,3,64]{1,3,2,0:T(8,128)}, u32[]{:S(2)}) copy-start(f32[1,1024,3,64]{1,3,2,0:T(8,128)} %copy-done.67) | copy-start | bytes 2359300
  509.3 103.9 %all-gather.27.cloned.1.call-start = ((), (), s32[]{:S(2)}) async-start(), calls=%async_computation.23 | async-start | bytes 1966080 | tf_op jit(solution)/shard_map/all_gather | solution.py:214
  575.6 4.2 collective-permute-start.2
  582.2 101.2 %reduce-scatter.30.cloned.1.call-start = ((), (), s32[]{:S(2)}) async-start(), calls=%async_computation.25 | async-start | bytes 3932160 | tf_op jit(solution)/shard_map/reduce_scatter | solution.py:261
  623.0 90.8 %reduce-scatter.28.cloned.1.call-start = ((), (), s32[]{:S(2)}) async-start(), calls=%async_computation.24 | async-start | bytes 3932160 | tf_op jit(solution)/shard_map/reduce_scatter | solution.py:260
  648.8 112.0 %all-gather.31.cloned.1.call-start = ((), (), s32[]{:S(2)}) async-start(), calls=%async_computation.27 | async-start | bytes 1966080 | tf_op jit(solution)/shard_map/all_gather | solution.py:214
  651.4 124.1 %copy-start.12 = (pred[512,1024]{1,0:T(8,128)(4,1)}, pred[512,1024]{1,0:T(8,128)(4,1)S(1)}, u32[]{:S(2)}) copy-start(pred[512,1024]{1,0:T(8,128)(4,1)S(1)} %get-tuple-element.212) | copy-start | bytes 1572868
  651.4 144.5 %copy-start.14 = (pred[512,1024]{1,0:T(8,128)(4,1)}, pred[512,1024]{1,0:T(8,128)(4,1)S(1)}, u32[]{:S(2)}) copy-start(pred[512,1024]{1,0:T(8,128)(4,1)S(1)} %get-tuple-element.213) | copy-start | bytes 1572868
  719.3 7.2 collective-permute-start.3
  728.9 134.9 %reduce-scatter.42.cloned.1.call-start = ((), (), s32[]{:S(2)}) async-start(), calls=%async_computation.36 | async-start | bytes 983040
  783.8 81.7 %reduce-scatter.40.cloned.1.call-start = ((), (), s32[]{:S(2)}) async-start(), calls=%async_computation.35 | async-start | bytes 2457600
  808.0 88.5 %reduce-scatter.34.cloned.1.call-start = ((), (), s32[]{:S(2)}) async-start(), calls=%async_computation.29 | async-start | bytes 3932160 | tf_op jit(solution)/shard_map/reduce_scatter | solution.py:261
  818.8 124.5 %reduce-scatter.32.cloned.1.call-start = ((), (), s32[]{:S(2)}) async-start(), calls=%async_computation.28 | async-start | bytes 3932160 | tf_op jit(solution)/shard_map/reduce_scatter | solution.py:260
  823.5 200.8 %reduce-scatter.22.cloned.1.call-start = ((), (), s32[]{:S(2)}) async-start(), calls=%async_computation.17 | async-start | bytes 3932160 | tf_op jit(solution)/shard_map/reduce_scatter | solution.py:188
  842.9 199.3 %reduce-scatter.36.cloned.1.call-start = ((), (), s32[]{:S(2)}) async-start(), calls=%async_computation.33 | async-start | bytes 2949120 | tf_op jit(solution)/shard_map/reduce_scatter | solution.py:367
  852.9 239.8 %reduce-scatter.38.cloned.1.call-start = ((), (), s32[]{:S(2)}) async-start(), calls=%async_computation.34 | async-start | bytes 2949120 | tf_op jit(solution)/shard_map/reduce_scatter | solution.py:368
  862.7 80.7 %copy-start.11 = (bf16[1,256,768]{2,1,0:T(8,128)(2,1)S(1)}, bf16[1,256,768]{2,1,0:T(8,128)(2,1)}, u32[]{:S(2)}) copy-start(bf16[1,256,768]{2,1,0:T(8,128)(2,1)} %get-tuple-element.106) | copy-start | bytes 1179652
  862.7 80.7 %copy-start.144 = (f32[256]{0:T(256)S(1)}, f32[256]{0:T(256)}, u32[]{:S(2)}) copy-start(f32[256]{0:T(256)} %copy-done.143) | copy-start | bytes 3076
  862.7 161.6 %copy-start.8 = (bf16[1,256,768]{2,1,0:T(8,128)(2,1)S(1)}, bf16[1,256,768]{2,1,0:T(8,128)(2,1)}, u32[]{:S(2)}) copy-start(bf16[1,256,768]{2,1,0:T(8,128)(2,1)} %bitcast_select_fusion.3) | copy-start | bytes 1179652
  862.7 161.6 %copy-start.51 = (bf16[1,256,768]{2,1,0:T(8,128)(2,1)S(1)}, bf16[1,256,768]{2,1,0:T(8,128)(2,1)}, u32[]{:S(2)}) copy-start(bf16[1,256,768]{2,1,0:T(8,128)(2,1)} %get-tuple-element.107) | copy-start | bytes 1179652
  862.7 161.6 %copy-start.128 = (f32[768]{0:T(1024)S(1)}, f32[768]{0:T(1024)}, u32[]{:S(2)}) copy-start(f32[768]{0:T(1024)} %copy-done.127) | copy-start | bytes 9220
  862.8 83.4 %copy-start.170 = (f32[256]{0:T(256)}, f32[256]{0:T(256)S(1)}, u32[]{:S(2)}) copy-start(f32[256]{0:T(256)S(1)} %add_rsqrt_fusion.6) | copy-start | bytes 3076
  (242 other events, 1913.1 us)
Sparse Core Ops, SparseCore 0:
  10.4 33.5 all-gather.32
  45.6 40.5 all-gather.34
  87.8 29.5 all-gather.36
  128.4 43.1 reduce-scatter.17
  176.7 30.8 all-gather.16
  234.5 43.8 reduce-scatter.19
  280.9 30.8 all-gather.22
  313.6 30.8 all-gather.28
  346.3 30.8 all-gather.18
  379.4 30.8 all-gather.20
  412.1 30.8 all-gather.24
  479.8 43.9 reduce-scatter.25
  526.7 43.8 reduce-scatter.23
  582.3 30.8 all-gather.26
  623.1 43.8 reduce-scatter.29
  669.9 43.8 reduce-scatter.27
  729.1 31.6 all-gather.30
  783.9 23.2 reduce-scatter.41
  809.5 41.0 reduce-scatter.39
  853.4 43.0 reduce-scatter.33
  899.4 43.8 reduce-scatter.31
  946.4 45.0 reduce-scatter.21
  994.4 47.7 reduce-scatter.35
  1044.9 47.6 reduce-scatter.37
where the time goes:
time: 1110 us; the launch traced here: 1100 us
  waiting for transfers between devices  543 us (49%)
  matrix products  232 us (21%)
  blocking collectives  140 us (13%)
  other arithmetic  106 us (10%)
  local copies, waits for them, and re-layouts  51.3 us (5%)
  between operations  18.4 us (2%)
    all_gather x6, waiting for transfers between devices, layer_pieces(): gathered = lax.all_gather(x_part, 'tensor', axis=1, tiled=True)  149 us
    reduce_scatter x3, waiting for transfers between devices, layer_backward(): lax.psum_scatter(attn_in_grad, 'tensor', scatter_dimension=1, tiled=True)  124 us
    reduce_scatter x3, waiting for transfers between devices, layer_forward(): summed = lax.psum_scatter(branch, 'tensor', scatter_dimension=1, tiled=True)  84 us
    psum x1, blocking collectives, body(): lax.psum((small_held[0], small_held[1], qv_full, up_full, small_held[4]),...  78.1 us
    all_gather x3, waiting for transfers between devices, layer_backward(): gradient_rows = lax.all_gather(grad_b, 'tensor', axis=1, tiled=True)  57.9 us
    reduce_scatter x1, waiting for transfers between devices, body(): lax.psum_scatter(matrix_grads[3], 'dp', scatter_dimension=1, tiled=True)  50.5 us
    reduce_scatter x3, waiting for transfers between devices, layer_backward(): lax.psum_scatter(feedforward_input_gradient, 'tensor', scatter_dimension=...  41.6 us
    all_gather x1, blocking collectives, fetch_weights(): lax.all_gather(shards[0], 'dp', axis=1, tiled=True)  40.9 us
  transfers between devices with their start and end apart: 28, of which 21 were waited for; matrix products, arithmetic and copies ran while one was open for 23% of the time, Pallas kernels for 0%

commit v1 on v0

v1 whole, which is shorter than its diff:
```python
import functools
import math

import jax
import jax.numpy as jnp
from jax import lax
from jax.experimental import pallas as pl
from jax.experimental.pallas import tpu as pltpu
from jax.sharding import PartitionSpec as P

HEAD_DIM = 64
ROT = 16
DOC_MOST = 384
QB = 256
EPS = 1e-05
ROOT_HALF = 0.7071067811865476
INV_ROOT_TAU = 0.3989422804014327
MASKED = -1e30
LANES = 128
SEC, DP, TEN = "section", "dp", "tensor"

F32 = jnp.float32
BF16 = jnp.bfloat16
MESH = pl.DeviceIdType.MESH
ANY = pl.ANY
VMEM_LIMIT = 62 * 1024 * 1024


def dot(a, b):
    return lax.dot_general(a, b, (((1,), (0,)), ((), ())), preferred_element_type=F32)


def dot_bt(a, b):
    return lax.dot_general(a, b, (((1,), (1,)), ((), ())), preferred_element_type=F32)


def dot_at(a, b):
    return lax.dot_general(a, b, (((0,), (0,)), ((), ())), preferred_element_type=F32)


def rows_of(index, size):
    return pl.ds(pl.multiple_of(index * size, size), size)


class Dims:
    def __init__(self, mesh_shape, inputs, segments, qkv, up):
        self.n_s = mesh_shape[SEC]
        self.n_z = mesh_shape[DP]
        self.n_t = mesh_shape[TEN]
        self.R = inputs[2]
        self.D = inputs[3]
        self.T = segments[2]
        self.HC = qkv[3]
        self.HP = -(-self.HC // 256) * 256
        self.NH = self.HC // HEAD_DIM
        self.FF = up[2]
        self.DW = qkv[2]
        self.NQ = self.T // QB
        self.k0 = [max(0, QB * (j + 1) - QB - DOC_MOST) for j in range(self.NQ)]
        self.kw = [QB * (j + 1) - self.k0[j] for j in range(self.NQ)]
        self.off = [sum(self.kw[:j]) for j in range(self.NQ)]
        self.KR = sum(self.kw)
        self.KM = max(self.kw)
        self.starts = [0, self.HP, 2 * self.HP]


class Place:
    def __init__(self, dm):
        self.s = lax.axis_index(SEC)
        self.z = lax.axis_index(DP)
        self.t = lax.axis_index(TEN)
        self.dm = dm

    def tensor_peer(self, k):
        return lax.rem(self.t + k, self.dm.n_t)

    def tensor_source(self, k):
        return lax.rem(self.t + self.dm.n_t - k, self.dm.n_t)

    def dp_peer(self, k):
        return lax.rem(self.z + k, self.dm.n_z)

    def dp_source(self, k):
        return lax.rem(self.z + self.dm.n_z - k, self.dm.n_z)

    def greet(self, dp):
        barrier = pltpu.get_barrier_semaphore()
        count = 0
        for k in range(1, self.dm.n_t):
            pl.semaphore_signal(
                barrier, inc=1, device_id={TEN: self.tensor_peer(k)}, device_id_type=MESH
            )
            count += 1
        if dp:
            for k in range(1, self.dm.n_z):
                pl.semaphore_signal(
                    barrier, inc=1, device_id={DP: self.dp_peer(k)}, device_id_type=MESH
                )
                count += 1
        pl.semaphore_signal(barrier, inc=1, device_id={SEC: 1 - self.s}, device_id_type=MESH)
        count += 1
        pl.semaphore_wait(barrier, count)


def remote(src, dst, send_sem, recv_sem, axis, peer):
    return pltpu.make_async_remote_copy(
        src_ref=src,
        dst_ref=dst,
        send_sem=send_sem,
        recv_sem=recv_sem,
        device_id={axis: peer},
        device_id_type=MESH,
    )


def unit_rows(values):
    centre = jnp.mean(values, axis=-1, keepdims=True)
    centred = values - centre
    inverse = lax.rsqrt(jnp.mean(centred * centred, axis=-1, keepdims=True) + EPS)
    return centred * inverse, inverse


def partner_lanes(values):
    width = values.shape[1]
    lane = lax.broadcasted_iota(jnp.int32, values.shape, 1) & (HEAD_DIM - 1)
    up = pltpu.roll(values, width - ROT // 2, 1)
    down = pltpu.roll(values, ROT // 2, 1)
    return jnp.where(lane < ROT // 2, up, down)


def norm_rows(dm, x_ref, a_ref, m_ref, n_ref, gain, shift, b):
    rows = rows_of(b, dm.R)
    unit, _ = unit_rows(x_ref[rows, :].astype(F32))
    n_ref[rows, :] = unit.astype(BF16)
    a_ref[rows, :] = (unit * gain[0:1, :] + shift[0:1, :]).astype(BF16)
    m_ref[rows, :] = (unit * gain[1:2, :] + shift[1:2, :]).astype(BF16)


def widen(dm, table):
    return jnp.concatenate([table] * (dm.HP // LANES), axis=1)


def rotary_tables(dm, ct_ref, st_ref):
    lane = lax.broadcasted_iota(jnp.int32, (QB, LANES), 1) & (HEAD_DIM - 1)
    order = (lane & (ROT // 2 - 1)).astype(F32)
    step = jnp.exp(order * (-2.0 * math.log(10000.0) / ROT))

    def body(b, carry):
        place = (lax.broadcasted_iota(jnp.int32, (QB, LANES), 0) + b * QB).astype(F32)
        angle = place * step
        sine = jnp.sin(angle)
        rows = rows_of(b, QB)
        ct_ref[rows, :] = jnp.where(lane < ROT, jnp.cos(angle), 1.0)
        st_ref[rows, :] = jnp.where(lane < ROT // 2, -sine, jnp.where(lane < ROT, sine, 0.0))
        return carry

    lax.fori_loop(0, dm.T // QB, body, 0)


def mask_bias(dm, seg_row, bias_ref):
    for j in range(dm.NQ):
        q0, k0, kw, off = QB * j, dm.k0[j], dm.kw[j], dm.off[j]
        query_seg = seg_row[:, q0 : q0 + QB]
        for i in range(kw // LANES):
            start = k0 + i * LANES
            key_seg = jnp.broadcast_to(seg_row[:, start : start + LANES], (QB, LANES)).T
            key = lax.broadcasted_iota(jnp.int32, (LANES, QB), 0) + start
            query = lax.broadcasted_iota(jnp.int32, (LANES, QB), 1) + q0
            allowed = (key_seg == query_seg) & (key <= query)
            bias_ref[off + i * LANES : off + (i + 1) * LANES, :] = jnp.where(allowed, 0.0, MASKED)


def project_rows(dm, a_ref, wqkv_ref, qvb, ct_ref, st_ref, q_ref, k_ref, v_ref, qt_ref, kt_ref, vt_ref, b):
    HP = dm.HP
    rows = rows_of(b, QB)
    acc = dot(a_ref[rows, :], wqkv_ref[...])
    ct, st = widen(dm, ct_ref[rows, :]), widen(dm, st_ref[rows, :])
    q = acc[:, 0:HP] + qvb[0:1, :]
    q = ((q * ct + partner_lanes(q) * st) * 0.125).astype(BF16)
    k = acc[:, HP : 2 * HP]
    k = (k * ct + partner_lanes(k) * st).astype(BF16)
    v = (acc[:, 2 * HP : 3 * HP] + qvb[1:2, :]).astype(BF16)
    q_ref[rows, :] = q
    k_ref[rows, :] = k
    v_ref[rows, :] = v
    qt_ref[:, rows] = q.T
    kt_ref[:, rows] = k.T
    vt_ref[:, rows] = v.T


def attend(dm, k_ref, qt_ref, qtm, vt_ref, bias_ref, pt_ref, ct_ref, c_ref):
    HP = dm.HP
    row = lax.broadcasted_iota(jnp.int32, (HP, QB), 0)
    ct_ref[...] = jnp.zeros_like(ct_ref)
    for j in range(dm.NQ):
        q0, k0, kw, off = QB * j, dm.k0[j], dm.kw[j], dm.off[j]
        for h in range(dm.NH):
            inside = (row >= h * HEAD_DIM) & (row < (h + 1) * HEAD_DIM)
            qtm[h] = jnp.where(inside, qt_ref[:, q0 : q0 + QB], jnp.zeros((HP, QB), BF16))

        def head(h, carry):
            hrows = rows_of(h, HEAD_DIM)
            scores = dot(k_ref[k0 : k0 + kw, :], qtm[h])
            scores = scores + bias_ref[off : off + kw, :]
            top = jnp.max(scores, axis=0, keepdims=True)
            probs = jnp.exp(scores - top)
            total = jnp.sum(probs, axis=0, keepdims=True)
            probs = (probs * (1.0 / total)).astype(BF16)
            pt_ref[off : off + kw, pl.ds(pl.multiple_of(h * QB, QB), QB)] = probs
            ct_ref[hrows, q0 : q0 + QB] = dot(vt_ref[hrows, k0 : k0 + kw], probs)
            return carry

        lax.fori_loop(0, dm.NH, head, 0)
        c_ref[q0 : q0 + QB, :] = ct_ref[:, q0 : q0 + QB].T.astype(BF16)


def hidden_rows(dm, m_ref, wup_ref, upb, h_ref, slope_ref, b):
    rows = rows_of(b, QB)
    u = dot(m_ref[rows, :], wup_ref[...]) + upb[...]
    cumulative = 0.5 * (1.0 + lax.erf(u * ROOT_HALF))
    h_ref[rows, :] = (u * cumulative).astype(BF16)
    slope_ref[rows, :] = (cumulative + u * INV_ROOT_TAU * jnp.exp(-0.5 * u * u)).astype(BF16)


def branch_rows(dm, c_ref, h_ref, wot_ref, wdt_ref, b):
    rows = rows_of(b, dm.R)
    return dot_bt(c_ref[rows, :], wot_ref[...]) + dot_bt(h_ref[rows, :], wdt_ref[...])


def pad_qkv(dm, raw_ref, out_ref):
    out_ref[...] = jnp.zeros_like(out_ref)
    for c in range(3):
        out_ref[:, c * dm.HP : c * dm.HP + dm.HC] = raw_ref[c]


def pad_heads(dm, raw_ref, out_ref):
    out_ref[...] = jnp.zeros_like(out_ref)
    out_ref[:, 0 : dm.HC] = raw_ref[...]


def small_width(dm):
    return max(dm.D, dm.FF, dm.HP)


def unpack_small(dm, ref):
    return (
        ref[0:2, 0 : dm.D],
        ref[2:4, 0 : dm.D],
        ref[6:8, 0 : dm.HP],
        ref[4:5, 0 : dm.FF],
        ref[5:6, 0 : dm.D],
    )


def pack_small(dm, t, gain, shift, qv, up, resid, out_ref):
    out_ref[...] = jnp.zeros_like(out_ref)
    out_ref[0:2, 0 : dm.D] = gain[...]
    out_ref[2:4, 0 : dm.D] = shift[...]
    out_ref[4:5, 0 : dm.FF] = up[:, pl.ds(pl.multiple_of(t * dm.FF, dm.FF), dm.FF)]
    out_ref[5:6, 0 : dm.D] = resid[...]
    for i in range(dm.n_t):

        @pl.when(t == i)
        def _(i=i):
            out_ref[6:8, 0 : dm.HC] = qv[:, i * dm.HC : (i + 1) * dm.HC]


def turn_shard(dm, wide, src, dst):
    rows, cols = src.shape
    whole_rows, whole_cols = -(-rows // QB) * QB, -(-cols // LANES) * LANES
    wide[0:whole_rows, 0:whole_cols] = jnp.zeros((whole_rows, whole_cols), wide.dtype)
    wide[0:rows, 0:cols] = src[...]
    for i in range(0, whole_rows, QB):
        n = min(QB, rows - i)
        dst[:, i : i + n] = wide[i : i + QB, 0:whole_cols].T[0:cols, 0:n]


def small_rows(dm):
    return (2, 8, small_width(dm))


def back_heads(dm, at, gb_ref, wot_ref, dc_ref, dct_ref):
    def body(b, carry):
        rows = rows_of(b, QB)
        grad = dot(gb_ref[rows, :], wot_ref[...]).astype(BF16)
        dc_ref[rows, :] = grad
        dct_ref[:, rows] = grad.T
        return carry

    lax.fori_loop(0, dm.T // QB, body, 0)


def attend_back(dm, q_ref, v_ref, kt_ref, pt_ref, dc_ref, dct_ref, qm, dcm, dctm, ds, dk_ref, dv_ref, dqt_ref):
    HP = dm.HP
    lane = lax.broadcasted_iota(jnp.int32, (QB, HP), 1)
    row = lax.broadcasted_iota(jnp.int32, (HP, QB), 0)
    dk_ref[...] = jnp.zeros_like(dk_ref)
    dv_ref[...] = jnp.zeros_like(dv_ref)
    dqt_ref[...] = jnp.zeros_like(dqt_ref)
    for j in range(dm.NQ):
        q0, k0, kw, off = QB * j, dm.k0[j], dm.kw[j], dm.off[j]
        for h in range(dm.NH):
            low, high = h * HEAD_DIM, (h + 1) * HEAD_DIM
            in_lane = (lane >= low) & (lane < high)
            in_row = (row >= low) & (row < high)
            zero = jnp.zeros((QB, HP), BF16)
            qm[h * QB : (h + 1) * QB, :] = jnp.where(in_lane, q_ref[q0 : q0 + QB, :], zero)
            dcm[h * QB : (h + 1) * QB, :] = jnp.where(in_lane, dc_ref[q0 : q0 + QB, :], zero)
            dctm[h] = jnp.where(in_row, dct_ref[:, q0 : q0 + QB], jnp.zeros((HP, QB), BF16))

        def head(h, carry):
            hrows = rows_of(h, HEAD_DIM)
            lanes = pl.ds(pl.multiple_of(h * QB, QB), QB)
            probs = pt_ref[off : off + kw, lanes].astype(F32)
            prob_grad = dot(v_ref[k0 : k0 + kw, :], dctm[h])
            mean = jnp.sum(probs * prob_grad, axis=0, keepdims=True)
            score = (probs * (prob_grad - mean)).astype(BF16)
            ds[0:kw, lanes] = score
            dqt_ref[hrows, q0 : q0 + QB] = dot(kt_ref[hrows, k0 : k0 + kw], score)
            return carry

        lax.fori_loop(0, dm.NH, head, 0)
        dv_ref[k0 : k0 + kw, :] += dot(pt_ref[off : off + kw, :], dcm[...])
        dk_ref[k0 : k0 + kw, :] += dot(ds[0:kw, :], qm[...])


def back_hidden(dm, r, gb_ref, acc):
    def body(b, carry):
        rows = rows_of(b, QB)
        du = dot(gb_ref[rows, :], r.wdt[...]) * r.slope[rows, :].astype(F32)
        acc[4:5, 0 : dm.FF] += jnp.sum(du, axis=0, keepdims=True)
        r.du[rows, :] = du.astype(BF16)
        return carry

    lax.fori_loop(0, dm.T // QB, body, 0)


def back_rows(dm, r, gain, acc, b):
    HP = dm.HP
    rows = rows_of(b, QB)
    unit = r.n[rows, :].astype(F32)
    dmid = dot_bt(r.du[rows, :], r.wup[...])
    acc[1:2, 0 : dm.D] += jnp.sum(dmid * unit, axis=0, keepdims=True)
    acc[3:4, 0 : dm.D] += jnp.sum(dmid, axis=0, keepdims=True)
    ct, st = widen(dm, r.ctab[rows, :]), widen(dm, r.stab[rows, :])
    dq = r.turned[:, rows].T
    dq = (dq * ct - partner_lanes(dq) * st) * 0.125
    acc[6:7, 0:HP] += jnp.sum(dq, axis=0, keepdims=True)
    r.dqkv[rows, 0:HP] = dq.astype(BF16)
    dk = r.dk[rows, :]
    r.dqkv[rows, HP : 2 * HP] = (dk * ct - partner_lanes(dk) * st).astype(BF16)
    dv = r.dv[rows, :]
    acc[7:8, 0:HP] += jnp.sum(dv, axis=0, keepdims=True)
    r.dqkv[rows, 2 * HP : 3 * HP] = dv.astype(BF16)
    datt = dot_bt(r.dqkv[rows, :], r.wqkv[...])
    acc[0:1, 0 : dm.D] += jnp.sum(datt * unit, axis=0, keepdims=True)
    acc[2:3, 0 : dm.D] += jnp.sum(datt, axis=0, keepdims=True)
    return datt * gain[0:1, :] + dmid * gain[1:2, :]


def weight_grad(dm, r, piece, gb_ref):
    def body(i, carry):
        cols = rows_of(i, QB)
        if piece == 0:
            made = dot_at(r.a[:, cols], r.dqkv[...])
            for c in range(3):
                r.wg[0][c, cols, :] = made[:, c * dm.HP : c * dm.HP + dm.HC].astype(BF16)
        elif piece == 1:
            r.wg[1][cols, :] = dot_at(r.m[:, cols], r.du[...]).astype(BF16)
        elif piece == 2:
            r.wg[2][cols, :] = dot_at(gb_ref[:, cols], r.c[...])[:, 0 : dm.HC].astype(BF16)
        else:
            r.wg[3][cols, :] = dot_at(gb_ref[:, cols], r.h[...]).astype(BF16)
        return carry

    lax.fori_loop(0, dm.D // QB, body, 0)


def norm_back(grad, values):
    unit, inverse = unit_rows(values)
    return inverse * (
        grad
        - jnp.mean(grad, axis=-1, keepdims=True)
        - unit * jnp.mean(grad * unit, axis=-1, keepdims=True)
    )


class Refs:
    pass


PIECES = range(4)
X0, GB1, Y0, X1, Y1, E1, GB0, E0, TS = CHANNELS = range(9)


def held_shapes(dm):
    T, D, HP, FF = dm.T, dm.D, dm.HP, dm.FF
    return dict(
        a=(T, D), m=(T, D), n=(T, D), h=(T, FF), slope=(T, FF), c=(T, HP), q=(T, HP), v=(T, HP), kt=(HP, T),
        pt=(dm.KR, dm.NH * QB), wqkv=(D, 3 * HP), wup=(D, FF), wot=(D, HP), wdt=(D, FF),
    )


def whole_shapes(dm):
    return [(3, dm.D, dm.HC), (dm.D, dm.FF), (dm.D, dm.HC), (dm.D, dm.FF)]


def part_shapes(dm):
    return [(3, dm.DW, dm.HC), (dm.DW, dm.FF), (dm.DW, dm.HC), (dm.DW, dm.FF)]


def out_layout(dm):
    S = jax.ShapeDtypeStruct
    block = S((dm.n_s, dm.R, dm.D), F32)
    return dict(
        o_y=block,
        o_g=block,
        o_w=[S(shape, F32) for shape in part_shapes(dm)],
        o_small=S((dm.n_t, 8, small_width(dm)), F32),
        land=[S(shape, BF16) for shape in whole_shapes(dm)],
        kept={name: S(shape, BF16) for name, shape in held_shapes(dm).items()},
    )


def scratch_layout(dm):
    T, D, R, HP, FF, HC, DW = dm.T, dm.D, dm.R, dm.HP, dm.FF, dm.HC, dm.DW
    NH, KR, KM, n_t, n_z = dm.NH, dm.KR, dm.KM, dm.n_t, dm.n_z
    W = small_width(dm)
    V, dma = pltpu.VMEM, pltpu.SemaphoreType.DMA
    raw, part = whole_shapes(dm), part_shapes(dm)
    rows = V((8, W), F32)
    peers = V((n_t - 1, R, D), BF16)
    layout = {name: V(shape, BF16) for name, shape in held_shapes(dm).items()}
    layout.update(
        x0=V((T, D), BF16), x1=V((T, D), BF16), gb1=V((T, D), BF16),
        raw_qkv=V(raw[0], BF16), raw_ot=V(raw[2], BF16), turn2=V(part[2], BF16),
        k=V((T, HP), BF16), vt=V((HP, T), BF16), bias=V((KR, QB), F32), turned=V((HP, T), F32),
        ctab=V((T, LANES), F32), stab=V((T, LANES), F32), small=V((2, 8, W), F32), small_own=rows,
        acc=V((2, 8, W), F32), core_sm=rows, own_sm=rows, dp_sm=V((n_z, 8, W), F32), row_sm=rows,
        all_sm=V((n_t, 8, W), F32),
        gown=V((R, D), F32), gb_own=V((R, D), BF16), yown=V((R, D), F32), x1_own=V((R, D), BF16),
        xo=V((R, D), BF16), eown=V((R, D), F32), ysend=peers, yrecv=peers, esend=peers, erecv=peers,
        du=V((T, FF), BF16), dc=V((T, HP), BF16), dct=V((HP, T), BF16),
        qm=V((NH * QB, HP), BF16), dcm=V((NH * QB, HP), BF16), dctm=V((NH, HP, QB), BF16),
        ds=V((KM, NH * QB), BF16), dk=V((T, HP), F32), dv=V((T, HP), F32), dqkv=V((T, 3 * HP), BF16),
        wg=[V(shape, BF16) for shape in raw],
        pg=[V(shape, BF16) for shape in raw],
        zrecv=[V((n_z - 1, *shape), BF16) for shape in part],
        zsum=[V(shape, F32) for shape in part],
        t_ss=dma((len(CHANNELS), n_t)), t_rs=dma((len(CHANNELS), n_t)),
        w_ss=dma((4, n_z)), w_rs=dma((4, n_z)), f_ss=dma((4, n_z)), f_rs=dma((4, n_z)),
        z_ss=dma((5, n_z)), z_rs=dma((5, n_z)),
        c_ss=dma((8,)), c_rs=dma((8,)),
        lsem=dma((12,)), osem=dma((32,)), isem=dma((40,)),
    )
    return layout


def input_layout():
    return dict(x_hbm=0, cot_hbm=0, raw0=1, raw1=1, raw2=1, raw3=1, seg=1, gain=1, shift=1, qv=1, up=1, resid=1)


SMALL, CORE_SUM, OUT_Y, OUT_G, HAND = range(5)
STAGE_SAVES = (("a", "m", "n", "q", "v", "kt", "wqkv"), ("pt", "c"), ("h", "slope", "wup"), ("wot", "wdt"))
PIECE_WAITS = (("q", "v", "kt", "wqkv", "pt", "c"), ("wup", "h", "slope"), ("wot",), ("wdt",))


def whole_step(dm, trees, *refs):
    r = Refs()
    counts = [tree.num_leaves for tree in trees]
    first = 0
    for tree, count in zip(trees, counts):
        r.__dict__.update(jax.tree.unflatten(tree, refs[first : first + count]))
        first += count
    at = Place(dm)
    s, z, t = at.s, at.z, at.t
    R, T, D, DW = dm.R, dm.T, dm.D, dm.DW
    n_t, n_z = dm.n_t, dm.n_z
    own_rows = rows_of(t, R)
    own_pieces = (r.raw0, r.raw1, r.turn2, r.raw3)
    first_slots = (r.raw_qkv, r.wup, r.raw_ot, r.wdt)
    second_slots = r.land

    def shard(ref, piece, index):
        rows = rows_of(index, DW)
        return ref.at[:, rows, :] if piece == 0 else ref.at[rows, :]

    saves, loads = {}, {}

    def save(src, dst, name):
        copy = pltpu.make_async_copy(src, dst, r.osem.at[len(saves)])
        copy.start()
        saves[name] = copy

    def load(src, dst, name):
        copy = pltpu.make_async_copy(src, dst, r.isem.at[len(loads)])
        copy.start()
        loads[name] = copy

    def to_peer(channel, src, dst, j):
        return remote(src, dst, r.t_ss.at[channel, j], r.t_rs.at[channel, j], TEN, at.tensor_peer(j))

    def spread_block(channel, src, land):
        for j in range(1, n_t):
            to_peer(channel, src, land.at[own_rows, :], j).start()

    def block_arrived(channel, src, land, j):
        to_peer(channel, src, land.at[rows_of(at.tensor_source(j), R), :], j).wait_recv()

    def spread_done(channel, src, land):
        for j in range(1, n_t):
            to_peer(channel, src, land.at[own_rows, :], j).wait_send()

    def to_other_core(channel, src, dst):
        return remote(src, dst, r.c_ss.at[channel], r.c_rs.at[channel], SEC, 1 - s)

    def weight_copy(piece, src, dst, j):
        return remote(src, dst, r.w_ss.at[piece, j], r.w_rs.at[piece, j], DP, at.dp_peer(j))

    def spread(piece, slots):
        for j in range(1, n_z):
            weight_copy(piece, own_pieces[piece], shard(slots[piece], piece, z), j).start()

    def forward_copy(piece, src, dst, index):
        return remote(src, dst, r.f_ss.at[piece, index], r.f_rs.at[piece, index], SEC, 1 - s)

    def pass_on(piece, slots, index, src):
        forward_copy(piece, src, shard(slots[piece], piece, index), index).start()

    def passed_on(piece):
        for j in range(n_z):
            forward_copy(piece, own_pieces[piece], own_pieces[piece], j).wait_send()

    def own_copy(piece, slots):
        return pltpu.make_async_copy(own_pieces[piece], shard(slots[piece], piece, z), r.lsem.at[2 + piece])

    def settle(slots, piece):
        for j in range(1, n_z):
            source = at.dp_source(j)
            landed = shard(slots[piece], piece, source)
            weight_copy(piece, own_pieces[piece], landed, j).wait_recv()
            pass_on(piece, slots, source, landed)
        own_copy(piece, slots).wait()

    def accept(slots, piece):
        for j in range(n_z):
            forward_copy(piece, own_pieces[piece], shard(slots[piece], piece, j), j).wait_recv()

    def ready(slots, layer, piece):
        @pl.when(s == layer)
        def _():
            settle(slots, piece)

        @pl.when(s != layer)
        def _():
            accept(slots, piece)

    def hand_over(piece):
        return to_other_core(HAND + piece, r.wg[piece], r.pg[piece])

    def z_copy(piece, j):
        return remote(
            shard(r.pg[piece], piece, at.dp_peer(j)), r.zrecv[piece].at[j - 1], r.z_ss.at[piece, j],
            r.z_rs.at[piece, j], DP, at.dp_peer(j),
        )

    def merge(piece):
        hand_over(piece).wait_recv()
        total = r.pg[piece][...].astype(F32) + r.wg[piece][...].astype(F32)
        r.pg[piece][...] = total.astype(BF16)
        for j in range(1, n_z):
            z_copy(piece, j).start()

    x_own = r.x_hbm.at[s, 0]
    load(x_own, r.x0.at[own_rows, :], "x0")
    load(r.cot_hbm.at[s, 0], r.gown, "gown")
    pack_small(dm, t, r.gain, r.shift, r.qv, r.up, r.resid, r.small_own)
    at.greet(True)
    spread_block(X0, x_own, r.x0)
    small_copy = to_other_core(SMALL, r.small_own, r.small.at[s])
    small_copy.start()
    load(r.small_own, r.small.at[s], "small")

    @pl.when(s == 0)
    def _():
        for piece in (0, 1):
            spread(piece, first_slots)
            own_copy(piece, first_slots).start()

    turn_shard(dm, r.dqkv, r.raw2, r.turn2)

    @pl.when(s == 0)
    def _():
        for piece in (2, 3):
            spread(piece, first_slots)
            own_copy(piece, first_slots).start()
        for piece in PIECES:
            pass_on(piece, first_slots, z, own_pieces[piece])

    @pl.when(s == 1)
    def _():
        for piece in PIECES:
            own_copy(piece, second_slots).start()

    r.acc[...] = jnp.zeros_like(r.acc)
    loads["gown"].wait()
    r.gb_own[...] = r.gown[...].astype(BF16)
    r.acc[1, 5:6, 0:D] = jnp.sum(r.gown[...], axis=0, keepdims=True)
    loads["small"].wait()
    to_other_core(SMALL, r.small_own, r.small.at[1 - s]).wait_recv()
    gain0, shift0, qvb0, upb0, resid0 = unpack_small(dm, r.small.at[0])
    loads["x0"].wait()
    norm_rows(dm, r.x0, r.a, r.m, r.n, gain0, shift0, t)
    spread_block(GB1, r.gb_own, r.gb1)
    load(r.gb_own, r.gb1.at[own_rows, :], "gb1")
    rotary_tables(dm, r.ctab, r.stab)
    mask_bias(dm, r.seg.at[s], r.bias)
    for j in range(1, n_t):
        block_arrived(X0, x_own, r.x0, j)
        norm_rows(dm, r.x0, r.a, r.m, r.n, gain0, shift0, at.tensor_source(j))

    def forward(params, arrive, after):
        gain, shift, qvb, upb, resid = params
        arrive(0)
        pad_qkv(dm, r.raw_qkv, r.wqkv)

        def project(b, carry):
            project_rows(dm, r.a, r.wqkv, qvb, r.ctab, r.stab, r.q, r.k, r.v, r.dct, r.kt, r.vt, b)
            return carry

        lax.fori_loop(0, T // QB, project, 0)
        after(0)
        attend(dm, r.k, r.dct, r.dctm, r.vt, r.bias, r.pt, r.turned, r.c)
        after(1)
        arrive(1)

        def hidden(b, carry):
            hidden_rows(dm, r.m, r.wup, upb, r.h, r.slope, b)
            return carry

        lax.fori_loop(0, T // QB, hidden, 0)
        after(2)
        arrive(2)
        pad_heads(dm, r.raw_ot, r.wot)
        arrive(3)
        after(3)

    def branches(x_ref, resid, send):
        def body(j, carry):
            r.ysend[j - 1] = branch_rows(dm, r.c, r.h, r.wot, r.wdt, at.tensor_peer(j)).astype(BF16)
            send(j)
            return carry

        lax.fori_loop(1, n_t, body, 0)
        r.yown[...] = (
            branch_rows(dm, r.c, r.h, r.wot, r.wdt, t) + x_ref[own_rows, :].astype(F32) + resid
        )

    def block_copy(channel, src, dst, j):
        return to_peer(channel, src.at[j - 1], dst.at[j - 1], j)

    def sum_blocks(channel, src, dst, total):
        for j in range(1, n_t):
            block_copy(channel, src, dst, j).wait_recv()
            total[...] += dst[j - 1].astype(F32)

    def sends_done(channel, src):
        for j in range(1, n_t):
            block_copy(channel, src, src, j).wait_send()

    def after_first(stage):
        for name in STAGE_SAVES[stage]:
            save(getattr(r, name), r.kept[name], name)

    forward((gain0, shift0, qvb0, upb0, resid0), lambda piece: ready(first_slots, 0, piece), after_first)

    @pl.when(s == 1)
    def _():
        for piece in PIECES:
            spread(piece, second_slots)
        for piece in PIECES:
            pass_on(piece, second_slots, z, own_pieces[piece])

    branches(r.x0, resid0, lambda j: block_copy(Y0, r.ysend, r.yrecv, j).start())
    sum_blocks(Y0, r.ysend, r.yrecv, r.yown)
    r.x1_own[...] = r.yown[...].astype(BF16)
    spread_block(X1, r.x1_own, r.x1)
    load(r.x1_own, r.x1.at[own_rows, :], "x1")

    def local_out(out, own, slot):
        return pltpu.make_async_copy(own, out.at[s], r.lsem.at[slot])

    def place(out, own, layer, channel):
        @pl.when(s == layer)
        def _():
            local_out(out, own, 6 + channel).start()

        @pl.when(s != layer)
        def _():
            to_other_core(channel, own, out.at[s]).start()

    def placed(out, own, layer, channel):
        @pl.when(s == layer)
        def _():
            local_out(out, own, 6 + channel).wait()

        @pl.when(s != layer)
        def _():
            to_other_core(channel, own, out.at[s]).wait_send()

    place(r.o_y, r.yown, 0, OUT_Y)

    gain1, shift1, qvb1, upb1, resid1 = unpack_small(dm, r.small.at[1])
    for name in STAGE_SAVES[0][:3]:
        saves[name].wait()
    loads["x1"].wait()
    norm_rows(dm, r.x1, r.a, r.m, r.n, gain1, shift1, t)
    for j in range(1, n_t):
        block_arrived(X1, r.x1_own, r.x1, j)
        norm_rows(dm, r.x1, r.a, r.m, r.n, gain1, shift1, at.tensor_source(j))

    def arrive_second(piece):
        ready(second_slots, 1, piece)
        for name in PIECE_WAITS[piece]:
            saves[name].wait()

        @pl.when(s == 0)
        def _():
            passed_on(piece)

        copy = pltpu.make_async_copy(second_slots[piece], first_slots[piece], r.isem.at[30 + piece])
        copy.start()
        copy.wait()

    forward((gain1, shift1, qvb1, upb1, resid1), arrive_second, lambda stage: None)
    sends_done(Y0, r.ysend)
    placed(r.o_y, r.yown, 0, OUT_Y)
    branches(r.x1, resid1, lambda j: None)

    def backward(layer, gb_ref, gain, early):
        acc = r.acc.at[layer]
        back_heads(dm, at, gb_ref, r.wot, r.dc, r.dct)
        back_hidden(dm, r, gb_ref, acc)
        early()
        attend_back(
            dm, r.q, r.v, r.kt, r.pt, r.dc, r.dct, r.qm, r.dcm, r.dctm, r.ds, r.dk, r.dv, r.turned
        )
        channel = (E0, E1)[layer]

        def body(j, carry):
            r.esend[j - 1] = back_rows(dm, r, gain, acc, at.tensor_peer(j)).astype(BF16)
            block_copy(channel, r.esend, r.erecv, j).start()
            return carry

        lax.fori_loop(1, n_t, body, 0)
        r.eown[...] = back_rows(dm, r, gain, acc, t)

    for j in range(1, n_t):
        block_arrived(GB1, r.gb_own, r.gb1, j)
    loads["gb1"].wait()
    backward(1, r.gb1, gain1, lambda: None)

    for piece in (3, 1, 0, 2):
        weight_grad(dm, r, piece, r.gb1)

        @pl.when(s == 0)
        def _(piece=piece):
            hand_over(piece).start()

    for name in r.kept:
        load(r.kept[name], getattr(r, name), name)
    load(x_own, r.xo, "xo")

    @pl.when(s == 1)
    def _():
        for piece in (3, 1, 0, 2):
            merge(piece)

    sum_blocks(E1, r.esend, r.erecv, r.eown)
    r.gown[...] += norm_back(r.eown[...], r.x1[own_rows, :].astype(F32))
    spread_done(GB1, r.gb_own, r.gb1)
    r.gb_own[...] = r.gown[...].astype(BF16)
    spread_block(GB0, r.gb_own, r.x0)
    load(r.gb_own, r.x0.at[own_rows, :], "gb0")
    for j in range(1, n_t):
        block_copy(Y1, r.ysend, r.yrecv, j).start()
    place(r.o_g, r.gown, 1, OUT_G)
    r.acc[0, 5:6, 0:D] = jnp.sum(r.gown[...], axis=0, keepdims=True)

    for name in r.kept:
        loads[name].wait()
    loads["gb0"].wait()
    for j in range(1, n_t):
        block_arrived(GB0, r.gb_own, r.x0, j)
    sends_done(E1, r.esend)

    def grad_piece(piece):
        @pl.when(s == 0)
        def _():
            hand_over(piece).wait_send()

        weight_grad(dm, r, piece, r.x0)

        @pl.when(s == 1)
        def _():
            hand_over(piece).start()

    def early():
        for piece in (3, 1, 2):
            grad_piece(piece)

        @pl.when(s == 0)
        def _():
            for piece in (3, 1, 2):
                merge(piece)

    backward(0, r.x0, gain0, early)

    core_copy = to_other_core(CORE_SUM, r.acc.at[1 - s], r.core_sm)
    core_copy.start()
    grad_piece(0)
    core_copy.wait_recv()
    r.own_sm[...] = r.acc[s] + r.core_sm[...]

    def dp_small(j):
        return remote(r.own_sm, r.dp_sm.at[j], r.z_ss.at[4, j], r.z_rs.at[4, j], DP, at.dp_peer(j))

    for j in range(1, n_z):
        dp_small(j).start()

    @pl.when(s == 0)
    def _():
        merge(0)

    sum_blocks(Y1, r.ysend, r.yrecv, r.yown)
    place(r.o_y, r.yown, 1, OUT_Y)
    total = r.own_sm[...]
    for j in range(1, n_z):
        dp_small(j).wait_recv()
        total = total + r.dp_sm[j]
    r.row_sm[...] = total

    def tensor_small(j, slot):
        return to_peer(TS, r.row_sm, r.all_sm.at[slot], j)

    for j in range(1, n_t):
        tensor_small(j, t).start()
    r.all_sm[t] = total

    sum_blocks(E0, r.esend, r.erecv, r.eown)
    placed(r.o_g, r.gown, 1, OUT_G)
    loads["xo"].wait()
    r.gown[...] += norm_back(r.eown[...], r.xo[...].astype(F32))
    place(r.o_g, r.gown, 0, OUT_G)
    for j in range(1, n_t):
        tensor_small(j, at.tensor_source(j)).wait_recv()
    save(r.all_sm, r.o_small, "small")

    for piece in (3, 1, 2, 0):
        kept = r.zsum[piece]
        kept[...] = shard(r.pg[piece], piece, z)[...].astype(F32)
        for j in range(1, n_z):
            z_copy(piece, j).wait_recv()
            kept[...] += r.zrecv[piece][j - 1].astype(F32)
        save(kept, r.o_w[piece], piece)

    for piece in PIECES:
        for j in range(1, n_z):
            z_copy(piece, j).wait_send()
            weight_copy(piece, own_pieces[piece], own_pieces[piece], j).wait_send()

        @pl.when(s == 1)
        def _(piece=piece):
            hand_over(piece).wait_send()
            passed_on(piece)

    small_copy.wait_send()
    core_copy.wait_send()
    for j in range(1, n_z):
        dp_small(j).wait_send()
    for j in range(1, n_t):
        tensor_small(j, t).wait_send()
    spread_done(X0, x_own, r.x0)
    spread_done(X1, r.x1_own, r.x1)
    spread_done(GB0, r.gb_own, r.x0)
    sends_done(Y1, r.ysend)
    sends_done(E0, r.esend)
    placed(r.o_y, r.yown, 1, OUT_Y)
    placed(r.o_g, r.gown, 0, OUT_G)
    to_other_core(OUT_Y, r.yown, r.o_y.at[1 - s]).wait_recv()
    to_other_core(OUT_G, r.gown, r.o_g.at[1 - s]).wait_recv()
    for piece in PIECES:
        saves[piece].wait()
    saves["small"].wait()


def run_step(dm, args):
    kinds = dict(input_layout())
    outs, scratch = out_layout(dm), scratch_layout(dm)
    out_leaves, out_tree = jax.tree.flatten(outs)
    scratch_leaves, scratch_tree = jax.tree.flatten(scratch)
    in_leaves, in_tree = jax.tree.flatten(kinds)
    vmem, anywhere = pl.BlockSpec(memory_space=pltpu.VMEM), pl.BlockSpec(memory_space=ANY)
    made = pl.pallas_call(
        functools.partial(whole_step, dm, (in_tree, out_tree, scratch_tree)),
        out_shape=out_leaves,
        in_specs=[vmem if kind else anywhere for kind in in_leaves],
        out_specs=[anywhere] * len(out_leaves),
        scratch_shapes=scratch_leaves,
        compiler_params=pltpu.CompilerParams(
            collective_id=0, has_side_effects=True, vmem_limit_bytes=VMEM_LIMIT
        ),
        name="whole_step",
    )(*jax.tree.leaves(args))
    return jax.tree.unflatten(out_tree, made)


def write_results(dm, y, g, w0, w1, w2, w3, small, *rest):
    oy, og, oqkv, oout, oup, odown, ogain, oshift, oqv, oupb, oresid = rest[:11]
    by, bg, bqkv, bup, b2, b3, wide, t2, sm, vgain, vshift, vqv, vupb, vresid, isem, osem = rest[11:]
    through = ((y, by, oy), (g, bg, og), (w0, bqkv, oqkv), (w1, bup, oup), (w3, b3, odown))
    into = [pltpu.make_async_copy(src, mid, isem.at[i]) for i, (src, mid, _) in enumerate(through)]
    into += [
        pltpu.make_async_copy(src, dst, isem.at[5 + i]) for i, (src, dst) in enumerate(((small, sm), (w2, b2)))
    ]
    for i in (5, 6, 0, 1, 2, 3, 4):
        into[i].start()
    out = []

    def leave(src, dst):
        copy = pltpu.make_async_copy(src, dst, osem.at[len(out)])
        copy.start()
        out.append(copy)

    into[5].wait()
    total = sm[0]
    for i in range(1, dm.n_t):
        total = total + sm[i]
    vgain[...] = total[0:2, 0 : dm.D]
    vshift[...] = total[2:4, 0 : dm.D]
    vresid[...] = total[5:6, 0 : dm.D]
    vqv[...] = jnp.concatenate([sm[i, 6:8, 0 : dm.HC] for i in range(dm.n_t)], axis=1)
    vupb[...] = jnp.concatenate([sm[i, 4:5, 0 : dm.FF] for i in range(dm.n_t)], axis=1)
    for src, dst in ((vgain, ogain), (vshift, oshift), (vresid, oresid), (vqv, oqv), (vupb, oupb)):
        leave(src, dst)
    into[6].wait()
    turn_shard(dm, wide, b2, t2)
    leave(t2, oout)
    for i, (_, mid, dst) in enumerate(through):
        into[i].wait()
        leave(mid, dst)
    for copy in out:
        copy.wait()


def run_results(dm, made):
    S, V, dma = jax.ShapeDtypeStruct, pltpu.VMEM, pltpu.SemaphoreType.DMA
    block, part = (dm.n_s, dm.R, dm.D), part_shapes(dm)
    turned = (dm.HC, dm.DW)
    pair, wide_up, one = (2, dm.D), (1, dm.n_t * dm.FF), (1, dm.D)
    heads = (2, dm.n_t * dm.HC)
    shapes = [block, block, part[0], turned, part[1], part[3], pair, pair, heads, wide_up, one]
    held = [block, block, part[0], part[1], part[2], part[3], (QB, max(dm.DW, dm.HP)), turned]
    held += [(dm.n_t, 8, small_width(dm)), pair, pair, heads, wide_up, one]
    anywhere = pl.BlockSpec(memory_space=ANY)
    return pl.pallas_call(
        functools.partial(write_results, dm),
        out_shape=[S(shape, F32) for shape in shapes],
        in_specs=[anywhere] * 7,
        out_specs=[anywhere] * 11,
        scratch_shapes=[V(shape, F32) for shape in held] + [dma((7,)), dma((11,))],
        compiler_params=pltpu.CompilerParams(vmem_limit_bytes=VMEM_LIMIT),
        name="write_results",
    )(made["o_y"], made["o_g"], *made["o_w"], made["o_small"])


def body(
    mesh_shape,
    inputs, segment_ids, cotangent, qkv_weight, out_weight, up_weight, down_weight,
    norm_gain, norm_bias, qv_bias, up_bias, resid_bias,
):
    dm = Dims(mesh_shape, inputs.shape, segment_ids.shape, qkv_weight.shape, up_weight.shape)
    made = run_step(
        dm,
        dict(
            x_hbm=inputs, cot_hbm=cotangent, raw0=qkv_weight[0], raw1=up_weight[0], raw2=out_weight[0],
            raw3=down_weight[0].T, seg=segment_ids, gain=norm_gain[0], shift=norm_bias[0], qv=qv_bias[0],
            up=up_bias, resid=resid_bias,
        ),
    )
    y, g, qkv, out, up, down, gain, shift, qv, upb, resid = run_results(dm, made)
    return (
        y[None, :, None], g[None, :, None], qkv[None], out[None], up[None], down.T[None],
        gain[None], shift[None], qv[None], upb, resid,
    )


def solution(mesh):
    rows = P(None, DP, TEN, None)
    both = P(SEC, None, DP, TEN, None)
    weights = (P(SEC, None, DP, TEN), P(SEC, TEN, DP), P(SEC, DP, TEN), P(SEC, TEN, DP))
    vectors = (P(SEC, None, None),) * 3 + (P(SEC, None),) * 2
    return jax.shard_map(
        functools.partial(body, dict(mesh.shape)),
        mesh=mesh,
        in_specs=(rows, P(None, DP, None), rows, *weights, *vectors),
        out_specs=(both, both, *weights, *vectors),
        check_vma=False,
    )
```

time: 1110 us -> 230 us (0.21)
  waiting for transfers between devices: 543 us -> 0 us
  matrix products: 232 us -> 0 us
  Pallas kernels: 0 us -> 226 us
  blocking collectives: 140 us -> 0 us
  other arithmetic: 106 us -> 0 us
  local copies, waits for them, and re-layouts: 51.3 us -> 0 us
  between operations: 18.4 us -> 0.86 us
    reduce_scatter x11 -> x0, waiting for transfers between devices: 313 us -> none  [the longest x3 124 us: layer_backward(): lax.psum_scatter(attn_in_grad, 'tensor', scatter_dimension=1, tiled=True)]
    pallas_call x0 -> x2, Pallas kernels: none -> 226 us  [the longest x1 222 us: run_step(): pl.pallas_call(functools.partial(whole_step, dm, (in_tree, out_tree, scra...]
    all_gather x11 -> x0, waiting for transfers between devices: 224 us -> none  [the longest x6 149 us: layer_pieces(): gathered = lax.all_gather(x_part, 'tensor', axis=1, tiled=True)]
    dot_general x81 -> x0, matrix products: 223 us -> none  [the longest x12 35.3 us: attend(): jnp.einsum('shqk,skhd->sqhd', probs_b, value_b, preferred_element_type=jn...]
    psum x1 -> x0, blocking collectives: 78.1 us -> none  [body(): lax.psum((small_held[0], small_held[1], qv_full, up_full, small_held[4]),...]
    all_gather x2 -> x0, blocking collectives: 62.2 us -> none  [the longest x1 40.9 us: fetch_weights(): lax.all_gather(shards[0], 'dp', axis=1, tiled=True)]
    reduce_sum x34 -> x0, other arithmetic: 57.3 us -> none  [the longest x8 18.6 us: attend(): jnp.sum(jnp.exp(scores - row_top), axis=-1, keepdims=True)]
    unnamed x531 -> x0, local copies, waits for them, and re-layouts: 33.3 us -> none
  transfers between devices with their start and end apart: 28 -> 0, of which waited for: 21 -> 0; matrix products, arithmetic and copies ran while one was open for 23% -> 0% of each run, Pallas kernels for 0% -> 0%
where the time goes in v1:
time: 230 us; the launch traced here: 227 us
  Pallas kernels  226 us (98%)
    pallas_call x1, Pallas kernels, run_step(): pl.pallas_call(functools.partial(whole_step, dm, (in_tree, out_tree, scra...  222 us

profile of v1, /device:TPU:0, one launch (start us, length us, event | category | flops | bytes accessed | tf_op | source)
XLA Modules:
  0.0 227.1 jit_solution(8242625144768197915)
XLA Ops:
  0.6 222.3 %whole_step.1 = (bf16[1024,768]{1,0:T(8,128)(2,1)}, bf16[1024,256]{1,0:T(8,128)(2,1)}, bf16[1024,768]{1,0:T(8,128)(2,1)}, bf16[256,1024]{1,0:T(8,128)(2,1)}, bf1...) custom-call(f32[2,1,256,768]{3,2,1,0:T(8,128)} %refs_0_.1, ...), custom_call_target="tpu_custom_call" | custom-call | tf_op jit(solution)/shard_map/whole_step/pallas_call | solution.py:904
  223.0 4.0 %write_results.1 = (f32[2,256,768]{2,1,0:T(8,128)}, f32[2,256,768]{2,1,0:T(8,128)}, f32[3,192,192]{2,1,0:T(8,128)}, f32[192,192]{1,0:T(8,128)}, f32[192,768]{1,0...) custom-call(f32[2,256,768]{2,1,0:T(8,128)} %get-tuple-element.29.y, ...), custom_call_target="tpu_custom_call" | custom-call | tf_op jit(solution)/shard_map/write_results/pallas_call | solution.py:966
